TPU v7x, 16 devices: a 4x2x1 block of a 4x4x8 slice. The times are simulated.
16 devices in a mesh: dp: 2 (over y, z), cp: 8 (over x, core).
Axes of the slice: x: 4, y: 2, z: 1, core: 2. Of those that a mesh axis runs over, the one named last changes fastest.
The devices are a block of a 4x4x8 slice.
Arguments:
- x_tok: bfloat16 [12288, 5120], P(('dp', 'cp')), parts along dimension 0
- w_q: bfloat16 [5120, 5120], replicated
- w_k: bfloat16 [5120, 5120], replicated
- w_v: bfloat16 [5120, 5120], replicated
- w_o: bfloat16 [5120, 5120], replicated
Outputs:
- output 1: bfloat16 [12288, 5120], P(('dp', 'cp')), parts along dimension 0
- output 2: bfloat16 [12288, 40, 128], P(('dp', 'cp')), parts along dimension 0
- output 3: bfloat16 [12288, 40, 128], P(('dp', 'cp')), parts along dimension 0
There are 2 independent parts. A program takes and returns all parts, laid end to end along the dimension named above; an argument that names none is the same for every part.
All inputs are finite; a program needn't handle non-finite values.
Results may differ from a plain program's by a relative error of at most 0.00883212.
Values are sent between devices in bfloat16 or wider.
A program may use at most 768 MiB of HBM per device.

v0:
```python
import math
import jax
import jax.numpy as jnp
from jax import lax
from jax.sharding import PartitionSpec as P

HEAD = 128
ROPE_BASE = 500000.0
NEG_BIG = -1e30
SCALE = 1.0 / math.sqrt(HEAD)


def rope_tables(tok_pos):
    inv_freq = 1.0 / (ROPE_BASE ** (jnp.arange(HEAD // 2, dtype=jnp.float32) * (2.0 / HEAD)))
    angles = tok_pos.astype(jnp.float32)[:, None] * inv_freq[None, :]
    return jnp.cos(angles)[:, None, :], jnp.sin(angles)[:, None, :]


def apply_rope(proj, rope_cos, rope_sin):
    first = proj[..., : HEAD // 2]
    second = proj[..., HEAD // 2:]
    return jnp.concatenate([first * rope_cos - second * rope_sin, second * rope_cos + first * rope_sin], axis=-1)


def local_positions(cp_rank, n_cp, half_len):
    offsets = jnp.arange(half_len, dtype=jnp.int32)
    return jnp.concatenate([cp_rank * half_len + offsets, (2 * n_cp - 1 - cp_rank) * half_len + offsets])


def project(x_loc, w_q, w_k, w_v, tok_pos):
    n_loc = x_loc.shape[0]
    n_heads = w_q.shape[1] // HEAD
    n_kv = w_k.shape[1] // HEAD
    rope_cos, rope_sin = rope_tables(tok_pos)
    q_loc = apply_rope(jnp.dot(x_loc, w_q, preferred_element_type=jnp.float32).reshape(n_loc, n_heads, HEAD), rope_cos, rope_sin).astype(jnp.bfloat16)
    k_loc = apply_rope(jnp.dot(x_loc, w_k, preferred_element_type=jnp.float32).reshape(n_loc, n_kv, HEAD), rope_cos, rope_sin).astype(jnp.bfloat16)
    v_loc = jnp.dot(x_loc, w_v, preferred_element_type=jnp.float32).astype(jnp.bfloat16).reshape(n_loc, n_kv, HEAD)
    return q_loc.reshape(n_loc, n_kv, n_heads // n_kv, HEAD), k_loc, v_loc


def attend_block(q_blk, k_blk, v_blk, keep_mask):
    scores = jnp.einsum('nkgh,mkh->nkgm', q_blk, k_blk, preferred_element_type=jnp.float32) * SCALE
    if keep_mask is not None:
        scores = jnp.where(keep_mask[:, None, None, :], scores, NEG_BIG)
    row_max = jnp.max(scores, axis=-1)
    weights = jnp.exp(scores - row_max[..., None])
    row_sum = jnp.sum(weights, axis=-1)
    attn_out = jnp.einsum('nkgm,mkh->nkgh', weights.astype(jnp.bfloat16), v_blk, preferred_element_type=jnp.float32)
    return attn_out / row_sum[..., None], row_max + jnp.log(row_sum)


def merge_parts(out_a, lse_a, out_b, lse_b):
    top_lse = jnp.maximum(lse_a, lse_b)
    wt_a = jnp.exp(lse_a - top_lse)
    wt_b = jnp.exp(lse_b - top_lse)
    wt_sum = wt_a + wt_b
    merged = (out_a * wt_a[..., None] + out_b * wt_b[..., None]) / wt_sum[..., None]
    return merged, top_lse + jnp.log(wt_sum)


def solution(mesh):
    n_cp = mesh.shape['cp']
    perm_next = [(src, (src + 1) % n_cp) for src in range(n_cp)]

    def per_device(x_loc, w_q, w_k, w_v, w_o):
        n_loc = x_loc.shape[0]
        half_len = n_loc // 2
        cp_rank = lax.axis_index('cp')
        tok_pos = local_positions(cp_rank, n_cp, half_len)
        q_loc, k_loc, v_loc = project(x_loc, w_q, w_k, w_v, tok_pos)
        keep_mask = tok_pos[:, None] >= tok_pos[None, :]
        attn_out, log_sum = attend_block(q_loc, k_loc, v_loc, keep_mask)
        pad_out = jnp.zeros((half_len,) + attn_out.shape[1:], jnp.float32)
        pad_lse = jnp.full((half_len,) + log_sum.shape[1:], NEG_BIG, jnp.float32)

        def kv_before(kv_cur):
            return attend_block(q_loc, kv_cur[0, :half_len], kv_cur[1, :half_len], None)

        def kv_after(kv_cur):
            part_out, part_lse = attend_block(q_loc[half_len:], kv_cur[0], kv_cur[1], None)
            return jnp.concatenate([pad_out, part_out]), jnp.concatenate([pad_lse, part_lse])

        def visit(step_idx, carry):
            attn_out, log_sum, kv_cur = carry
            kv_cur = lax.ppermute(kv_cur, 'cp', perm_next)
            src_rank = (cp_rank - step_idx) % n_cp
            part_out, part_lse = lax.cond(src_rank < cp_rank, kv_before, kv_after, kv_cur)
            attn_out, log_sum = merge_parts(attn_out, log_sum, part_out, part_lse)
            return attn_out, log_sum, kv_cur

        attn_out, log_sum, _ = lax.fori_loop(1, n_cp, visit, (attn_out, log_sum, jnp.stack([k_loc, v_loc])))
        y_loc = jnp.dot(attn_out.reshape(n_loc, -1).astype(jnp.bfloat16), w_o, preferred_element_type=jnp.float32).astype(jnp.bfloat16)
        return y_loc, k_loc, v_loc

    row_spec = P(('dp', 'cp'), None)
    kv_spec = P(('dp', 'cp'), None, None)
    full_spec = P(None, None)
    return jax.shard_map(per_device, mesh=mesh, in_specs=(row_spec, full_spec, full_spec, full_spec, full_spec), out_specs=(row_spec, kv_spec, kv_spec), check_vma=False)
```

profile of v0, /device:TPU:112, one launch (start us, length us, event | category | flops | bytes accessed | tf_op | source)
XLA Modules:
  0.0 2463.3 jit_solution(17180316475410382229)
XLA Ops:
  2.5 49.4 %convolution_bitcast_fusion = f32[96,8,40,128]{3,1,2,0:T(8,128)} fusion(bf16[768,5120]{1,0:T(8,128)(2,1)} %param.9, bf16[5120,5120]{1,0:T(8,128)(2,1)} %param.10), kind=kOutput, calls=%fused_computation.58 | convolution fusion | flops 40265318400 | bytes 76021760 | tf_op jit(solution)/shard_map/dot_general | solution.py:35
  66.5 49.6 %convolution_bitcast_fusion.1 = f32[96,8,40,128]{3,1,2,0:T(8,128)} fusion(bf16[768,5120]{1,0:T(8,128)(2,1)} %param.9, bf16[5120,5120]{1,0:T(8,128)(2,1)} %param.11), kind=kOutput, calls=%fused_computation.59 | convolution fusion | flops 40265318400 | bytes 76021760 | tf_op jit(solution)/shard_map/dot_general | solution.py:36
  130.7 44.5 %fusion.58 = (f32[768,40,64]{2,1,0:T(8,128)}, f32[768,40,64]{2,1,0:T(8,128)}, f32[768,40,64]{2,1,0:T(8,128)}, f32[768,40,64]{2,1,0:T(8,128)}) fusion(f32[768,40,128]{2,1,0:T(8,128)} %bitcast.150, f32[768,40,128]{2,1,0:T(8,128)} %bitcast.151), kind=kLoop, calls=%fused_computation.82 | loop fusion | bytes 62914560 | tf_op jit(solution)/shard_map/slice | solution.py:20
  176.7 38.3 %subtract_convert_fusion = (bf16[768,40,64]{2,0,1:T(8,128)(2,1)}, bf16[768,40,64]{2,0,1:T(8,128)(2,1)}, bf16[768,40,64]{2,0,1:T(8,128)(2,1)}, bf16[768,40,64]{2,0,1:T(8,128)(2,1)}) fusion(f32[768,40,64]{2,1,0:T(8,128)} %get-tuple-element.216, f32[768,40,64]{2,1,0:T(8,128)} %get-tuple-element.215, f32[768,64]{1,0:T(8,128)S(1)} %get-tuple-element.222, ...), kind=kLoop, calls=%fused_computation.55 | loop fusion | flops 31457280 | bytes 47579136 | tf_op jit(solution)/shard_map/convert.8
  227.9 39.5 %fusion.41 = (f32[768,40]{0,1:T(8,128)S(1)}, f32[40,768,768]{2,1,0:T(8,128)}) fusion(pred[768,768]{0,1:T(8,128)(4,1)S(1)} %copy-done.1, bf16[768,40,128]{2,0,1:T(8,128)(2,1)} %pad_maximum_fusion.1, bf16[768,40,64]{2,0,1:T(8,128)(2,1)} %get-tuple-element.212, bf16[768,40,64]{2,0,1:T(8,128)(2,1)} %get-tuple-element.211), kind=kOutput, calls=%fused_computation.48 | convolution fusion | flops 6126274560 | bytes 110813184 | tf_op jit(solution)/shard_map/nkgh,mkh->nkgm/dot_general | solution.py:42
  267.5 29.5 %fusion.39 = f32[768,40]{0,1:T(8,128)S(1)} fusion(f32[40,768,768]{2,1,0:T(8,128)} %get-tuple-element.226, f32[768,40]{0,1:T(8,128)S(1)} %get-tuple-element.225, pred[768,768]{0,1:T(8,128)(4,1)S(1)} %copy-done.1), kind=kLoop, calls=%fused_computation.46 | loop fusion | flops 94341120 | bytes 95207424 | tf_op jit(solution)/shard_map/reduce_sum | solution.py:47
  297.0 49.2 %convolution_convert_fusion.1 = bf16[768,5120]{1,0:T(8,128)(2,1)} fusion(bf16[768,5120]{1,0:T(8,128)(2,1)} %param.9, bf16[5120,5120]{1,0:T(8,128)(2,1)} %param.12), kind=kOutput, calls=%fused_computation.61 | convolution fusion | flops 40269250560 | bytes 68157440 | tf_op jit(solution)/shard_map/dot_general | solution.py:37
  346.2 42.3 %bitcast_divide_fusion.2 = f32[768,40,1,128]{0,3,1,2:T(8,128)} fusion(f32[40,768,768]{2,1,0:T(8,128)} %get-tuple-element.226, f32[768,40]{0,1:T(8,128)S(1)} %get-tuple-element.225, pred[768,768]{0,1:T(8,128)(4,1)S(1)} %copy-done.1, f32[768,40]{0,1:T(8,128)S(1)} %fusion.39, bf16[768,5120]{1,0:T(8,128)(2,1)} %convolution_convert_fusion.1), kind=kOutput, calls=%fused_computation.53 | convolution fusion | flops 6138101760 | bytes 118800384 | tf_op jit(solution)/shard_map/nkgm,mkh->nkgh/dot_general | solution.py:48
  449.9 1942.6 %while.19 = (s32[]{:T(128)}, f32[768,40,1,128]{3,0,1,2:T(8,128)}, f32[768,40,1]{0,1,2:T(8,128)S(1)}, bf16[2,768,40,128]{3,1,2,0:T(8,128)(2,1)}, s32[]{:T(128)}, ...) while((s32[]{:T(128)}, f32[768,40,1,128]{3,0,1,2:T(8,128)}, ...), condition=%wide.region_9.10_spmd, body=%wide.region_2.9_spmd.sunk | while | flops 6153953280 | bytes 336015680 | solution.py:91
  450.1 173.1 %collective-permute-done = bf16[2,768,40,128]{3,1,2,0:T(8,128)(2,1)} collective-permute-done((bf16[2,768,40,128]{3,1,2,0:T(8,128)(2,1)}, bf16[2,768,40,128]{3,1,2,0:T(8,128)(2,1)}, u32[]{:S(2)}, u32[]{:S(2)}) %collective-permute-start) | collective-permute-done | bytes 15728672 | tf_op jit(solution)/shard_map/while/body/eval_jaxpr/ppermute | solution.py:85
  623.3 73.0 %conditional.2 = (f32[768,40,1,128]{3,0,1,2:T(8,128)}, f32[768,40,1]{0,1,2:T(8,128)S(1)}) conditional(s32[]{:T(128)} %convert_element_type.83, (bf16[2,768,40,128]{3,1,2,0:T(8,128)(2,1)}, bf16[768,40,1,128]{3,0,1,2:T(8,128)(2,1)}) %tuple.72, (bf16[2,768,40,128]{3,1,2,0:T(8,128)(2,1)}, bf16[768,40,1,128]{3,0,1,2:T(8,128)(2,1)}) %tuple.72), branch_computations={%region_3.5_spmd, %region_6.8_spmd} | conditional | flops 6138071040 | bytes 193351696 | solution.py:87
  727.9 172.7 %collective-permute-done = bf16[2,768,40,128]{3,1,2,0:T(8,128)(2,1)} collective-permute-done((bf16[2,768,40,128]{3,1,2,0:T(8,128)(2,1)}, bf16[2,768,40,128]{3,1,2,0:T(8,128)(2,1)}, u32[]{:S(2)}, u32[]{:S(2)}) %collective-permute-start) | collective-permute-done | bytes 15728672 | tf_op jit(solution)/shard_map/while/body/eval_jaxpr/ppermute | solution.py:85
  900.7 73.0 %conditional.2 = (f32[768,40,1,128]{3,0,1,2:T(8,128)}, f32[768,40,1]{0,1,2:T(8,128)S(1)}) conditional(s32[]{:T(128)} %convert_element_type.83, (bf16[2,768,40,128]{3,1,2,0:T(8,128)(2,1)}, bf16[768,40,1,128]{3,0,1,2:T(8,128)(2,1)}) %tuple.72, (bf16[2,768,40,128]{3,1,2,0:T(8,128)(2,1)}, bf16[768,40,1,128]{3,0,1,2:T(8,128)(2,1)}) %tuple.72), branch_computations={%region_3.5_spmd, %region_6.8_spmd} | conditional | flops 6138071040 | bytes 193351696 | solution.py:87
  1005.3 172.7 %collective-permute-done = bf16[2,768,40,128]{3,1,2,0:T(8,128)(2,1)} collective-permute-done((bf16[2,768,40,128]{3,1,2,0:T(8,128)(2,1)}, bf16[2,768,40,128]{3,1,2,0:T(8,128)(2,1)}, u32[]{:S(2)}, u32[]{:S(2)}) %collective-permute-start) | collective-permute-done | bytes 15728672 | tf_op jit(solution)/shard_map/while/body/eval_jaxpr/ppermute | solution.py:85
  1178.1 73.0 %conditional.2 = (f32[768,40,1,128]{3,0,1,2:T(8,128)}, f32[768,40,1]{0,1,2:T(8,128)S(1)}) conditional(s32[]{:T(128)} %convert_element_type.83, (bf16[2,768,40,128]{3,1,2,0:T(8,128)(2,1)}, bf16[768,40,1,128]{3,0,1,2:T(8,128)(2,1)}) %tuple.72, (bf16[2,768,40,128]{3,1,2,0:T(8,128)(2,1)}, bf16[768,40,1,128]{3,0,1,2:T(8,128)(2,1)}) %tuple.72), branch_computations={%region_3.5_spmd, %region_6.8_spmd} | conditional | flops 6138071040 | bytes 193351696 | solution.py:87
  1282.7 172.7 %collective-permute-done = bf16[2,768,40,128]{3,1,2,0:T(8,128)(2,1)} collective-permute-done((bf16[2,768,40,128]{3,1,2,0:T(8,128)(2,1)}, bf16[2,768,40,128]{3,1,2,0:T(8,128)(2,1)}, u32[]{:S(2)}, u32[]{:S(2)}) %collective-permute-start) | collective-permute-done | bytes 15728672 | tf_op jit(solution)/shard_map/while/body/eval_jaxpr/ppermute | solution.py:85
  1455.4 73.0 %conditional.2 = (f32[768,40,1,128]{3,0,1,2:T(8,128)}, f32[768,40,1]{0,1,2:T(8,128)S(1)}) conditional(s32[]{:T(128)} %convert_element_type.83, (bf16[2,768,40,128]{3,1,2,0:T(8,128)(2,1)}, bf16[768,40,1,128]{3,0,1,2:T(8,128)(2,1)}) %tuple.72, (bf16[2,768,40,128]{3,1,2,0:T(8,128)(2,1)}, bf16[768,40,1,128]{3,0,1,2:T(8,128)(2,1)}) %tuple.72), branch_computations={%region_3.5_spmd, %region_6.8_spmd} | conditional | flops 6138071040 | bytes 193351696 | solution.py:87
  1560.1 172.7 %collective-permute-done = bf16[2,768,40,128]{3,1,2,0:T(8,128)(2,1)} collective-permute-done((bf16[2,768,40,128]{3,1,2,0:T(8,128)(2,1)}, bf16[2,768,40,128]{3,1,2,0:T(8,128)(2,1)}, u32[]{:S(2)}, u32[]{:S(2)}) %collective-permute-start) | collective-permute-done | bytes 15728672 | tf_op jit(solution)/shard_map/while/body/eval_jaxpr/ppermute | solution.py:85
  1732.8 73.0 %conditional.2 = (f32[768,40,1,128]{3,0,1,2:T(8,128)}, f32[768,40,1]{0,1,2:T(8,128)S(1)}) conditional(s32[]{:T(128)} %convert_element_type.83, (bf16[2,768,40,128]{3,1,2,0:T(8,128)(2,1)}, bf16[768,40,1,128]{3,0,1,2:T(8,128)(2,1)}) %tuple.72, (bf16[2,768,40,128]{3,1,2,0:T(8,128)(2,1)}, bf16[768,40,1,128]{3,0,1,2:T(8,128)(2,1)}) %tuple.72), branch_computations={%region_3.5_spmd, %region_6.8_spmd} | conditional | flops 6138071040 | bytes 193351696 | solution.py:87
  1837.5 172.7 %collective-permute-done = bf16[2,768,40,128]{3,1,2,0:T(8,128)(2,1)} collective-permute-done((bf16[2,768,40,128]{3,1,2,0:T(8,128)(2,1)}, bf16[2,768,40,128]{3,1,2,0:T(8,128)(2,1)}, u32[]{:S(2)}, u32[]{:S(2)}) %collective-permute-start) | collective-permute-done | bytes 15728672 | tf_op jit(solution)/shard_map/while/body/eval_jaxpr/ppermute | solution.py:85
  2010.2 73.0 %conditional.2 = (f32[768,40,1,128]{3,0,1,2:T(8,128)}, f32[768,40,1]{0,1,2:T(8,128)S(1)}) conditional(s32[]{:T(128)} %convert_element_type.83, (bf16[2,768,40,128]{3,1,2,0:T(8,128)(2,1)}, bf16[768,40,1,128]{3,0,1,2:T(8,128)(2,1)}) %tuple.72, (bf16[2,768,40,128]{3,1,2,0:T(8,128)(2,1)}, bf16[768,40,1,128]{3,0,1,2:T(8,128)(2,1)}) %tuple.72), branch_computations={%region_3.5_spmd, %region_6.8_spmd} | conditional | flops 6138071040 | bytes 193351696 | solution.py:87
  2114.9 172.7 %collective-permute-done = bf16[2,768,40,128]{3,1,2,0:T(8,128)(2,1)} collective-permute-done((bf16[2,768,40,128]{3,1,2,0:T(8,128)(2,1)}, bf16[2,768,40,128]{3,1,2,0:T(8,128)(2,1)}, u32[]{:S(2)}, u32[]{:S(2)}) %collective-permute-start) | collective-permute-done | bytes 15728672 | tf_op jit(solution)/shard_map/while/body/eval_jaxpr/ppermute | solution.py:85
  2287.6 73.0 %conditional.2 = (f32[768,40,1,128]{3,0,1,2:T(8,128)}, f32[768,40,1]{0,1,2:T(8,128)S(1)}) conditional(s32[]{:T(128)} %convert_element_type.83, (bf16[2,768,40,128]{3,1,2,0:T(8,128)(2,1)}, bf16[768,40,1,128]{3,0,1,2:T(8,128)(2,1)}) %tuple.72, (bf16[2,768,40,128]{3,1,2,0:T(8,128)(2,1)}, bf16[768,40,1,128]{3,0,1,2:T(8,128)(2,1)}) %tuple.72), branch_computations={%region_3.5_spmd, %region_6.8_spmd} | conditional | flops 6138071040 | bytes 193351696 | solution.py:87
  2404.7 49.8 %convolution_convert_fusion = bf16[768,5120]{1,0:T(8,128)(2,1)} fusion(bf16[768,5120]{0,1:T(8,128)(2,1)} %bitcast.161, bf16[5120,5120]{1,0:T(8,128)(2,1)} %param.13), kind=kOutput, calls=%fused_computation.60 | convolution fusion | flops 40269250560 | bytes 68157440 | tf_op jit(solution)/shard_map/dot_general | solution.py:92
  (97 shorter events, 859.8 us)
Async XLA Ops:
  130.7 44.5 %copy-start.2 = (f32[768]{0:T(1024)S(1)}, f32[768]{0:T(1024)}, u32[]{:S(2)}) copy-start(f32[768]{0:T(1024)} %get-tuple-element.224) | copy-start | bytes 9220
  215.0 12.9 copy-start.1
  404.5 17.4 slice-start
  413.5 8.5 slice-start.1
  450.0 173.2 %collective-permute-start = (bf16[2,768,40,128]{3,1,2,0:T(8,128)(2,1)}, bf16[2,768,40,128]{3,1,2,0:T(8,128)(2,1)}, u32[]{:S(2)}, u32[]{:S(2)}) collective-permute-start(bf16[2,768,40,128]{3,1,2,0:T(8,128)(2,1)} %get-tuple-element.297), channel_id=1, source_target_pairs={{0,1},{1,2},{2,3},{3,4},{4,5},{5,6},{6,7},{7,0},{8,9},{9,10},{10,1... | collective-permute-start | bytes 47185928 | tf_op jit(solution)/shard_map/while/body/eval_jaxpr/ppermute | solution.py:85
  727.9 172.7 %collective-permute-start = (bf16[2,768,40,128]{3,1,2,0:T(8,128)(2,1)}, bf16[2,768,40,128]{3,1,2,0:T(8,128)(2,1)}, u32[]{:S(2)}, u32[]{:S(2)}) collective-permute-start(bf16[2,768,40,128]{3,1,2,0:T(8,128)(2,1)} %get-tuple-element.297), channel_id=1, source_target_pairs={{0,1},{1,2},{2,3},{3,4},{4,5},{5,6},{6,7},{7,0},{8,9},{9,10},{10,1... | collective-permute-start | bytes 47185928 | tf_op jit(solution)/shard_map/while/body/eval_jaxpr/ppermute | solution.py:85
  1005.3 172.7 %collective-permute-start = (bf16[2,768,40,128]{3,1,2,0:T(8,128)(2,1)}, bf16[2,768,40,128]{3,1,2,0:T(8,128)(2,1)}, u32[]{:S(2)}, u32[]{:S(2)}) collective-permute-start(bf16[2,768,40,128]{3,1,2,0:T(8,128)(2,1)} %get-tuple-element.297), channel_id=1, source_target_pairs={{0,1},{1,2},{2,3},{3,4},{4,5},{5,6},{6,7},{7,0},{8,9},{9,10},{10,1... | collective-permute-start | bytes 47185928 | tf_op jit(solution)/shard_map/while/body/eval_jaxpr/ppermute | solution.py:85
  1282.7 172.7 %collective-permute-start = (bf16[2,768,40,128]{3,1,2,0:T(8,128)(2,1)}, bf16[2,768,40,128]{3,1,2,0:T(8,128)(2,1)}, u32[]{:S(2)}, u32[]{:S(2)}) collective-permute-start(bf16[2,768,40,128]{3,1,2,0:T(8,128)(2,1)} %get-tuple-element.297), channel_id=1, source_target_pairs={{0,1},{1,2},{2,3},{3,4},{4,5},{5,6},{6,7},{7,0},{8,9},{9,10},{10,1... | collective-permute-start | bytes 47185928 | tf_op jit(solution)/shard_map/while/body/eval_jaxpr/ppermute | solution.py:85
  1560.1 172.7 %collective-permute-start = (bf16[2,768,40,128]{3,1,2,0:T(8,128)(2,1)}, bf16[2,768,40,128]{3,1,2,0:T(8,128)(2,1)}, u32[]{:S(2)}, u32[]{:S(2)}) collective-permute-start(bf16[2,768,40,128]{3,1,2,0:T(8,128)(2,1)} %get-tuple-element.297), channel_id=1, source_target_pairs={{0,1},{1,2},{2,3},{3,4},{4,5},{5,6},{6,7},{7,0},{8,9},{9,10},{10,1... | collective-permute-start | bytes 47185928 | tf_op jit(solution)/shard_map/while/body/eval_jaxpr/ppermute | solution.py:85
  1837.5 172.7 %collective-permute-start = (bf16[2,768,40,128]{3,1,2,0:T(8,128)(2,1)}, bf16[2,768,40,128]{3,1,2,0:T(8,128)(2,1)}, u32[]{:S(2)}, u32[]{:S(2)}) collective-permute-start(bf16[2,768,40,128]{3,1,2,0:T(8,128)(2,1)} %get-tuple-element.297), channel_id=1, source_target_pairs={{0,1},{1,2},{2,3},{3,4},{4,5},{5,6},{6,7},{7,0},{8,9},{9,10},{10,1... | collective-permute-start | bytes 47185928 | tf_op jit(solution)/shard_map/while/body/eval_jaxpr/ppermute | solution.py:85
  2114.9 172.7 %collective-permute-start = (bf16[2,768,40,128]{3,1,2,0:T(8,128)(2,1)}, bf16[2,768,40,128]{3,1,2,0:T(8,128)(2,1)}, u32[]{:S(2)}, u32[]{:S(2)}) collective-permute-start(bf16[2,768,40,128]{3,1,2,0:T(8,128)(2,1)} %get-tuple-element.297), channel_id=1, source_target_pairs={{0,1},{1,2},{2,3},{3,4},{4,5},{5,6},{6,7},{7,0},{8,9},{9,10},{10,1... | collective-permute-start | bytes 47185928 | tf_op jit(solution)/shard_map/while/body/eval_jaxpr/ppermute | solution.py:85
  2404.7 49.9 %copy-start = (bf16[768,40,128]{2,0,1:T(8,128)(2,1)S(1)}, bf16[768,40,128]{2,0,1:T(8,128)(2,1)}, u32[]{:S(2)}) copy-start(bf16[768,40,128]{2,0,1:T(8,128)(2,1)} %pad_maximum_fusion.1) | copy-start | bytes 23592964
where the time goes:
time: 2470 us; the launch traced here: 2460 us
  waiting for transfers between devices  1210 us (49%)
  matrix products  582 us (24%)
  other arithmetic  374 us (15%)
  local copies, waits for them, and re-layouts  296 us (12%)
    ppermute x7, waiting for transfers between devices, visit(): kv_cur = lax.ppermute(kv_cur, 'cp', perm_next)  1210 us
    dot_general x8, matrix products, attend_block(): jnp.einsum('nkgm,mkh->nkgh', weights.astype(jnp.bfloat16), v_blk, preferr...  199 us
    dot_general x8, matrix products, attend_block(): jnp.einsum('nkgh,mkh->nkgm', q_blk, k_blk, preferred_element_type=jnp.flo...  185 us
    reduce_sum x8, other arithmetic, attend_block(): row_sum = jnp.sum(weights, axis=-1)  163 us
    div x7, other arithmetic, merge_parts(): (out_a * wt_a[..., None] + out_b * wt_b[..., None]) / wt_sum[..., None]  128 us
    while x7, local copies, waits for them, and re-layouts  93.1 us
    concatenate x7, local copies, waits for them, and re-layouts, kv_after(): jnp.concatenate([pad_out, part_out])  74.8 us
    dot_general x1, matrix products, per_device(): jnp.dot(attn_out.reshape(n_loc, -1).astype(jnp.bfloat16), w_o, preferred_...  49.8 us
  transfers between devices with their start and end apart: 7, of which 7 were waited for; matrix products, arithmetic and copies ran while one was open for 0% of the time, Pallas kernels for 0%

commit v1 on v0

v1 whole, which is shorter than its diff:
```python
import functools
import math

import jax
import jax.numpy as jnp
from jax import lax
from jax.experimental import pallas as pl
from jax.experimental.pallas import tpu as pltpu
from jax.sharding import PartitionSpec as P

HEAD = 128
ROPE_BASE = 500000.0
NEG_BIG = -1e30
EXP2_SCALE = math.log2(math.e) / math.sqrt(HEAD)
BQ = 1024
STREAM = 256
BK = 512
ROW_STEP = 256
LANES = 2 * HEAD
OUT_COLS = 512
MESH = pl.DeviceIdType.MESH


def rope_tables(tok_pos):
    inv_freq = 1.0 / (ROPE_BASE ** (jnp.arange(HEAD // 2, dtype=jnp.float32) * (2.0 / HEAD)))
    angles = tok_pos.astype(jnp.float32)[:, None] * inv_freq[None, :]
    cos, sin = jnp.cos(angles), jnp.sin(angles)
    return jnp.concatenate([cos, cos], axis=1), jnp.concatenate([-sin, sin], axis=1)


def local_positions(cp_rank, n_cp, half_len):
    offsets = jnp.arange(half_len, dtype=jnp.int32)
    return jnp.concatenate([cp_rank * half_len + offsets, (2 * n_cp - 1 - cp_rank) * half_len + offsets])


def layer_kernel(n_cp, n_chunk, x_hbm, wq_hbm, wk_hbm, wv_hbm, wo_hbm, cos_ref, sin_ref,
                 y_hbm, kp_hbm, vp_hbm, send_hbm, got_hbm, ogot_hbm,
                 x_scr, w_scr, h_scr, q_scr, k_scr, v_scr, vt_scr, o_scr, acc_scr, ml_scr, mx_scr, s0_scr, s1_scr,
                 oc_scr, wo_scr, y_scr, ys_scr,
                 x_sem, w_sem, h_sem, send_sem, recv_sem, in_sem, oself_sem, osend_sem, orecv_sem, oc_sem, wo_sem, ys_sem):
    me = lax.axis_index('cp')
    n_chip = n_cp // 2
    chip = lax.div(me, 2)
    n_loc = x_scr.shape[0]
    half_len = n_loc // 2
    seq = n_loc * n_cp
    n_pieces = 2 * n_cp
    n_stream = BQ // STREAM
    n_out = y_scr.shape[1] // OUT_COLS
    depth = n_cp * HEAD

    barrier = pltpu.get_barrier_semaphore()
    for other in range(n_cp):
        @pl.when(me != other)
        def _():
            pl.semaphore_signal(barrier, inc=1, device_id={'cp': other}, device_id_type=MESH)
    pl.semaphore_wait(barrier, n_cp - 1)

    def dest_chip(step):
        return lax.rem(chip + step + 1, n_chip)

    def w_copy(g, step, t):
        col = pl.multiple_of((g * n_chip + dest_chip(step)) * LANES, LANES)
        return pltpu.make_async_copy((wq_hbm, wk_hbm, wv_hbm)[t].at[:, pl.ds(col, LANES)], w_scr.at[t], w_sem.at[t])

    x_copy = pltpu.make_async_copy(x_hbm, x_scr, x_sem)
    x_copy.start()
    for t in range(3):
        w_copy(0, 0, t).start()
    y_scr[...] = jnp.zeros_like(y_scr)
    x_copy.wait()

    def to_peer(g, dest):
        return pltpu.make_async_remote_copy(
            src_ref=send_hbm.at[g, dest], dst_ref=got_hbm.at[g, me], send_sem=send_sem.at[g, dest],
            recv_sem=recv_sem.at[g, me], device_id={'cp': dest}, device_id_type=MESH)

    def from_peer(g, src):
        return pltpu.make_async_remote_copy(
            src_ref=send_hbm.at[g, src], dst_ref=got_hbm.at[g, src], send_sem=send_sem.at[g, src],
            recv_sem=recv_sem.at[g, src], device_id={'cp': src}, device_id_type=MESH)

    def spill(g, step, i):
        par = lax.rem(step, 2)
        dest = 2 * dest_chip(step) + i
        col = pl.ds(pl.multiple_of((g * n_cp + dest) * HEAD, HEAD), HEAD)
        mine = pltpu.make_async_copy(h_scr.at[par, i], got_hbm.at[g, dest], h_sem.at[par, i, 0])
        other = pltpu.make_async_copy(h_scr.at[par, i], send_hbm.at[g, dest], h_sem.at[par, i, 0])
        plain = [pltpu.make_async_copy(h_scr.at[par, i, 1], kp_hbm.at[:, col], h_sem.at[par, i, 1]),
                 pltpu.make_async_copy(h_scr.at[par, i, 2], vp_hbm.at[:, col], h_sem.at[par, i, 2])]
        return dest, mine, other, plain

    def spill_start(g, step):
        for i in range(2):
            dest, mine, other, plain = spill(g, step, i)

            @pl.when(dest == me)
            def _():
                mine.start()

            @pl.when(dest != me)
            def _():
                other.start()
            for copy in plain:
                copy.start()

    def spill_send(g, step):
        for i in range(2):
            dest, mine, other, plain = spill(g, step, i)

            @pl.when(dest == me)
            def _():
                mine.wait()

            @pl.when(dest != me)
            def _():
                other.wait()
                to_peer(g, dest).start()
            for copy in plain:
                copy.wait()

    def project(g):
        @pl.loop(0, n_chip)
        def _(step):
            par = lax.rem(step, 2)
            for t in range(3):
                w_copy(g, step, t).wait()
                prod = jnp.dot(x_scr[...], w_scr[t], preferred_element_type=jnp.float32)
                for i in range(2):
                    head = prod[:, i * HEAD:(i + 1) * HEAD]
                    if t < 2:
                        head = head * cos_ref[...] + pltpu.roll(head, HEAD // 2, 1) * sin_ref[...]
                    h_scr[par, i, t] = head.astype(jnp.bfloat16)
                later = g * n_chip + step + 1

                @pl.when(later < n_chunk * n_chip)
                def _():
                    w_copy(lax.div(later, n_chip), lax.rem(later, n_chip), t).start()
                if t == 0:
                    @pl.when(step > 0)
                    def _():
                        spill_send(g, step - 1)
            spill_start(g, step)
        spill_send(g, n_chip - 1)

    def home(piece):
        return (piece, 0) if piece < n_cp else (n_pieces - 1 - piece, 1)

    def rows_of(piece):
        return pl.ds(piece * half_len, half_len)

    def load(g, piece):
        src, half = home(piece)
        return [pltpu.make_async_copy(got_hbm.at[g, src, t, pl.ds(half * half_len, half_len)], dst.at[rows_of(piece)], in_sem.at[piece, t])
                for t, dst in enumerate((q_scr, k_scr, v_scr))]

    def o_send(g, piece):
        dest, half = home(piece)
        par = lax.rem(g, 2)
        return pltpu.make_async_remote_copy(
            src_ref=o_scr.at[par, rows_of(piece)], dst_ref=ogot_hbm.at[g, me, pl.ds(half * half_len, half_len)],
            send_sem=osend_sem.at[par, piece], recv_sem=orecv_sem.at[g, me, half], device_id={'cp': dest}, device_id_type=MESH)

    def o_keep(g, piece):
        dest, half = home(piece)
        return pltpu.make_async_copy(o_scr.at[lax.rem(g, 2), rows_of(piece)], ogot_hbm.at[g, dest, pl.ds(half * half_len, half_len)], oself_sem.at[half])

    def o_recv(g, src, half):
        return pltpu.make_async_remote_copy(
            src_ref=o_scr.at[0, pl.ds(0, half_len)], dst_ref=ogot_hbm.at[g, src, pl.ds(half * half_len, half_len)],
            send_sem=osend_sem.at[0, 0], recv_sem=orecv_sem.at[g, src, half], device_id={'cp': src}, device_id_type=MESH)

    def o_sent(g):
        for piece in range(n_pieces):
            @pl.when(home(piece)[0] != me)
            def _():
                o_send(g, piece).wait_send()

    def scores(u, q_u, k_base, s_scr, slot, off):
        cols = slice(u * STREAM, (u + 1) * STREAM)
        top = None
        for r in range(0, BK, ROW_STEP):
            k_blk = k_scr[pl.ds(k_base + r, ROW_STEP), :]
            s = lax.dot_general(k_blk, q_u, (((1,), (1,)), ((), ())), preferred_element_type=jnp.float32)
            if off is not None and off - r < ROW_STEP - 1:
                key_at = lax.broadcasted_iota(jnp.int32, s.shape, 0)
                query_at = lax.broadcasted_iota(jnp.int32, s.shape, 1)
                s = jnp.where(key_at <= query_at + (off - r), s, NEG_BIG)
            s_scr[r:r + ROW_STEP, cols] = s
            blk_top = jnp.max(s, axis=0, keepdims=True)
            top = blk_top if top is None else jnp.maximum(top, blk_top)
        mx_scr[slot:slot + 1, cols] = top

    def fold(u, k_base, s_scr, slot, first):
        cols = slice(u * STREAM, (u + 1) * STREAM)
        m_new = mx_scr[slot:slot + 1, cols]
        if not first:
            m_old = ml_scr[0:1, cols]
            m_new = jnp.maximum(m_old, m_new)
        shift = m_new * EXP2_SCALE
        p = jnp.exp2(s_scr[:, cols] * EXP2_SCALE - shift)
        l_blk = jnp.sum(p, axis=0, keepdims=True)
        pv = jnp.dot(vt_scr[:, pl.ds(k_base, BK)], p.astype(jnp.bfloat16), preferred_element_type=jnp.float32)
        if first:
            ml_scr[1:2, cols] = l_blk
            acc_scr[:, cols] = pv
        else:
            alpha = jnp.exp2(m_old * EXP2_SCALE - shift)
            ml_scr[1:2, cols] = ml_scr[1:2, cols] * alpha + l_blk
            acc_scr[:, cols] = acc_scr[:, cols] * alpha + pv
        ml_scr[0:1, cols] = m_new

    def diag_off(u, b):
        off = u * STREAM - b * BK
        return None if off >= BK - 1 else off

    def attend(g):
        @pl.when(g >= 2)
        def _():
            o_sent(g - 2)
        for src in range(n_cp):
            @pl.when(me != src)
            def _():
                from_peer(g, src).wait_recv()
        for piece in range(n_pieces):
            for copy in load(g, piece):
                copy.start()
        par = lax.rem(g, 2)

        @pl.loop(0, seq // BQ)
        def _(qi):
            q_base = pl.multiple_of(qi * BQ, BQ)
            for i in range(seq // BQ):
                @pl.when(qi == i)
                def _():
                    for piece in range(-(-i * BQ // half_len), -(-(i + 1) * BQ // half_len)):
                        for copy in load(g, piece):
                            copy.wait()

            for r in range(0, BQ, BK):
                rows = pl.ds(pl.multiple_of(q_base + r, BK), BK)
                vt_scr[:, rows] = v_scr[rows, :].T
            q_u = [q_scr[pl.ds(q_base + u * STREAM, STREAM), :] for u in range(n_stream)]
            diag0, diag1 = q_base, pl.multiple_of(q_base + BK, BK)
            for u in range(n_stream):
                scores(u, q_u[u], diag0, s0_scr, 0, diag_off(u, 0))
            for u in range(n_stream):
                if (u + 1) * STREAM > BK:
                    scores(u, q_u[u], diag1, s1_scr, 1, diag_off(u, 1))
                fold(u, diag0, s0_scr, 0, True)
            for u in range(n_stream):
                scores(u, q_u[u], 0, s0_scr, 0, None)
                if (u + 1) * STREAM > BK:
                    fold(u, diag1, s1_scr, 1, False)

            @pl.loop(0, qi)
            def _(t):
                blk0 = pl.multiple_of(t * (2 * BK), 2 * BK)
                blk1, blk2 = pl.multiple_of(blk0 + BK, BK), pl.multiple_of(blk0 + 2 * BK, BK)
                for u in range(n_stream):
                    scores(u, q_u[u], blk1, s1_scr, 1, None)
                    fold(u, blk0, s0_scr, 0, False)
                for u in range(n_stream):
                    scores(u, q_u[u], blk2, s0_scr, 0, None)
                    fold(u, blk1, s1_scr, 1, False)

            for u in range(n_stream):
                cols = slice(u * STREAM, (u + 1) * STREAM)
                out = acc_scr[:, cols] / ml_scr[1:2, cols]
                o_scr[par, pl.ds(q_base + u * STREAM, STREAM), :] = out.T.astype(jnp.bfloat16)
            for i in range(seq // BQ):
                @pl.when(qi == i)
                def _():
                    for piece in range(i * BQ // half_len, (i + 1) * BQ // half_len):
                        @pl.when(home(piece)[0] == me)
                        def _():
                            o_keep(g, piece).start()

                        @pl.when(home(piece)[0] != me)
                        def _():
                            o_send(g, piece).start()
        for piece in range(n_pieces):
            @pl.when(home(piece)[0] == me)
            def _():
                o_keep(g, piece).wait()

    def wo_copy(g, nb, slot):
        rows = pl.ds(pl.multiple_of(g * depth, depth), depth)
        return pltpu.make_async_copy(wo_hbm.at[rows, pl.ds(pl.multiple_of(nb * OUT_COLS, OUT_COLS), OUT_COLS)], wo_scr.at[slot], wo_sem.at[slot])

    def y_copy(nb, slot):
        return pltpu.make_async_copy(ys_scr.at[slot], y_hbm.at[:, pl.ds(pl.multiple_of(nb * OUT_COLS, OUT_COLS), OUT_COLS)], ys_sem.at[slot])

    def combine(g):
        wo_copy(g, 0, 0).start()
        wo_copy(g, 1, 1).start()
        for src in range(n_cp):
            @pl.when(me != src)
            def _():
                for half in range(2):
                    o_recv(g, src, half).wait_recv()
        loads = [pltpu.make_async_copy(ogot_hbm.at[g, h], oc_scr.at[:, pl.ds(h * HEAD, HEAD)], oc_sem.at[h]) for h in range(n_cp)]
        for copy in loads:
            copy.start()
        for copy in loads:
            copy.wait()

        @pl.loop(0, n_out)
        def _(nb):
            slot = lax.rem(nb, 2)
            cols = pl.ds(pl.multiple_of(nb * OUT_COLS, OUT_COLS), OUT_COLS)
            wo_copy(g, nb, slot).wait()
            y_scr[:, cols] += jnp.dot(oc_scr[...], wo_scr[slot], preferred_element_type=jnp.float32)

            @pl.when(nb + 2 < n_out)
            def _():
                wo_copy(g, nb + 2, slot).start()

            @pl.when(g == n_chunk - 1)
            def _():
                @pl.when(nb >= 2)
                def _():
                    y_copy(nb - 2, slot).wait()
                ys_scr[slot] = y_scr[:, cols].astype(jnp.bfloat16)
                y_copy(nb, slot).start()

    @pl.loop(0, n_chunk + 4)
    def _(i):
        @pl.when(i < n_chunk)
        def _():
            project(i)

        @pl.when(jnp.logical_and(i >= 2, i < n_chunk + 2))
        def _():
            attend(i - 2)

        @pl.when(i >= 4)
        def _():
            combine(i - 4)

    for nb in range(n_out - 2, n_out):
        y_copy(nb, nb % 2).wait()
    for g in range(max(n_chunk - 2, 0), n_chunk):
        o_sent(g)

    @pl.loop(0, n_chunk)
    def _(g):
        for dest in range(n_cp):
            @pl.when(me != dest)
            def _():
                to_peer(g, dest).wait_send()


def layer(x_loc, w_q, w_k, w_v, w_o, cos, sin, n_cp):
    n_loc, d_model = x_loc.shape
    width = w_q.shape[1]
    n_chunk = width // HEAD // n_cp
    seq = n_loc * n_cp
    bf16, f32 = jnp.bfloat16, jnp.float32
    shape = jax.ShapeDtypeStruct
    hbm = pl.BlockSpec(memory_space=pltpu.HBM)
    vmem = pl.BlockSpec(memory_space=pltpu.VMEM)
    dma = pltpu.SemaphoreType.DMA
    rows = pltpu.VMEM((seq, HEAD), bf16)
    stats = pltpu.VMEM((8, BQ), f32)
    score = pltpu.VMEM((BK, BQ), f32)
    pieces = shape((n_chunk, n_cp, 3, n_loc, HEAD), bf16)
    y, k_plain, v_plain, *_ = pl.pallas_call(
        functools.partial(layer_kernel, n_cp, n_chunk),
        in_specs=[hbm] * 5 + [vmem] * 2,
        out_specs=[hbm] * 6,
        out_shape=[shape((n_loc, w_o.shape[1]), bf16), shape((n_loc, width), bf16), shape((n_loc, width), bf16),
                   pieces, pieces, shape((n_chunk, n_cp, n_loc, HEAD), bf16)],
        scratch_shapes=[
            pltpu.VMEM((n_loc, d_model), bf16), pltpu.VMEM((3, d_model, LANES), bf16), pltpu.VMEM((2, 2, 3, n_loc, HEAD), bf16),
            rows, rows, rows, pltpu.VMEM((HEAD, seq), bf16), pltpu.VMEM((2, seq, HEAD), bf16), pltpu.VMEM((HEAD, BQ), f32),
            stats, stats, score, score,
            pltpu.VMEM((n_loc, n_cp * HEAD), bf16), pltpu.VMEM((2, n_cp * HEAD, OUT_COLS), bf16), pltpu.VMEM((n_loc, w_o.shape[1]), f32),
            pltpu.VMEM((2, n_loc, OUT_COLS), bf16),
            dma, dma((3,)), dma((2, 2, 3)), dma((n_chunk, n_cp)), dma((n_chunk, n_cp)), dma((2 * n_cp, 3)), dma((2,)),
            dma((2, 2 * n_cp)), dma((n_chunk, n_cp, 2)), dma((n_cp,)), dma((2,)), dma((2,))],
        compiler_params=pltpu.CompilerParams(collective_id=0, has_side_effects=True, vmem_limit_bytes=62 << 20),
        name="layer",
    )(x_loc, w_q, w_k, w_v, w_o, cos, sin)
    return y, k_plain, v_plain


def solution(mesh):
    n_cp = mesh.shape['cp']

    def per_device(x_loc, w_q, w_k, w_v, w_o):
        n_loc = x_loc.shape[0]
        cos, sin = rope_tables(local_positions(lax.axis_index('cp'), n_cp, n_loc // 2))
        y_loc, k_plain, v_plain = layer(x_loc, w_q, w_k, w_v, w_o, cos, sin, n_cp)
        return y_loc, k_plain.reshape(n_loc, -1, HEAD), v_plain.reshape(n_loc, -1, HEAD)

    row_spec = P(('dp', 'cp'), None)
    kv_spec = P(('dp', 'cp'), None, None)
    full_spec = P(None, None)
    return jax.shard_map(per_device, mesh=mesh, in_specs=(row_spec, full_spec, full_spec, full_spec, full_spec), out_specs=(row_spec, kv_spec, kv_spec), check_vma=False)
```

time: 2470 us -> 462 us (0.19)
  waiting for transfers between devices: 1210 us -> 0 us
  matrix products: 582 us -> 0 us
  Pallas kernels: 0 us -> 436 us
  other arithmetic: 374 us -> 3.31 us
  local copies, waits for them, and re-layouts: 296 us -> 21.1 us
    ppermute x7 -> x0, waiting for transfers between devices: 1210 us -> none  [visit(): kv_cur = lax.ppermute(kv_cur, 'cp', perm_next)]
    dot_general x20 -> x0, matrix products: 582 us -> none  [the longest x8 199 us: attend_block(): jnp.einsum('nkgm,mkh->nkgh', weights.astype(jnp.bfloat16), v_blk, preferr...]
    pallas_call x0 -> x1, Pallas kernels: none -> 436 us  [layer(): pl.pallas_call(functools.partial(layer_kernel, n_cp, n_chunk), in_specs=[...]
    reduce_sum x8 -> x0, other arithmetic: 163 us -> none  [attend_block(): row_sum = jnp.sum(weights, axis=-1)]
    div x7 -> x0, other arithmetic: 128 us -> none  [merge_parts(): (out_a * wt_a[..., None] + out_b * wt_b[..., None]) / wt_sum[..., None]]
    while x9 -> x0, local copies, waits for them, and re-layouts: 121 us -> none
    concatenate x14 -> x0, local copies, waits for them, and re-layouts: 74.8 us -> none  [the longest x7 74.8 us: kv_after(): jnp.concatenate([pad_out, part_out])]
    another operation x2 -> x0, other arithmetic: 53.3 us -> none
  transfers between devices with their start and end apart: 7 -> 0, of which waited for: 7 -> 0; matrix products, arithmetic and copies ran while one was open for 0% -> 0% of each run, Pallas kernels for 0% -> 0%
where the time goes in v1:
time: 462 us; the launch traced here: 461 us
  Pallas kernels  436 us (94%)
  local copies, waits for them, and re-layouts  21.1 us (5%)
    pallas_call x1, Pallas kernels, layer(): pl.pallas_call(functools.partial(layer_kernel, n_cp, n_chunk), in_specs=[...  436 us
    unnamed x7, local copies, waits for them, and re-layouts  21.1 us

profile of v1, /device:TPU:112, one launch (start us, length us, event | category | flops | bytes accessed | tf_op | source)
XLA Modules:
  0.0 461.4 jit_solution(17488838325128306841)
XLA Ops:
  0.7 1.4 fusion
  2.1 0.9 pad_maximum_fusion.1.sin_ref
  3.1 0.9 pad_maximum_fusion.cos_ref
  4.0 436.3 %layer.1 = (bf16[768,5120]{1,0:T(8,128)(2,1)}, bf16[768,5120]{1,0:T(8,128)(2,1)}, bf16[768,5120]{1,0:T(8,128)(2,1)}, bf16[5,8,3,768,128]{4,3,2,1,0:T(8,128)(2,1)...) custom-call(bf16[768,5120]{1,0:T(8,128)(2,1)} %x_hbm.1, bf16[5120,5120]{1,0:T(8,128)(2,1)} %wq_hbm.1, ...), custom_call_target="tpu_custom_call" | custom-call | tf_op jit(solution)/shard_map/layer/pallas_call | solution.py:368
  440.3 0.0 slice-start
  440.3 8.9 %copy.8 = bf16[96,8,40,128]{3,2,1,0:T(8,128)(2,1)} copy(bf16[96,8,40,128]{3,1,2,0:T(8,128)(2,1)} %bitcast.9) | data formatting | bytes 15728640
  449.2 0.0 slice-start.1
  449.2 8.9 %copy.9 = bf16[96,8,40,128]{3,2,1,0:T(8,128)(2,1)} copy(bf16[96,8,40,128]{3,1,2,0:T(8,128)(2,1)} %bitcast.7) | data formatting | bytes 15728640
  458.2 0.0 slice-done
  458.2 0.0 slice-done.1
  458.2 3.2 copy.11
  (4 shorter events, 0.0 us)
Async XLA Ops:
  440.3 17.9 %slice-start = ((s8[7864320]{0:T(1024)(128)(4,1)}), s8[4194304]{0:T(1024)(128)(4,1)S(1)}, s32[]{:S(2)}) async-start(s8[7864320]{0:T(1024)(128)(4,1)} %bitcast.4), calls=%async_computation | async-start | bytes 8388608
  449.2 8.9 %slice-start.1 = ((s8[7864320]{0:T(1024)(128)(4,1)}), s8[3670016]{0:T(1024)(128)(4,1)S(1)}, s32[]{:S(2)}) async-start(s8[7864320]{0:T(1024)(128)(4,1)} %bitcast.4), calls=%async_computation.1 | async-start | bytes 7340032

commit v2 on v1

--- a/solution.py
+++ b/solution.py
@@ -17,15 +17,17 @@
 BK = 512
 ROW_STEP = 256
 LANES = 2 * HEAD
-OUT_COLS = 512
+OUT_COLS = 1024
+COPY_ROWS = 128
 MESH = pl.DeviceIdType.MESH
 
 
 def rope_tables(tok_pos):
-    inv_freq = 1.0 / (ROPE_BASE ** (jnp.arange(HEAD // 2, dtype=jnp.float32) * (2.0 / HEAD)))
+    lane = jnp.arange(HEAD, dtype=jnp.int32)
+    inv_freq = 1.0 / (ROPE_BASE ** ((lane % (HEAD // 2)).astype(jnp.float32) * (2.0 / HEAD)))
     angles = tok_pos.astype(jnp.float32)[:, None] * inv_freq[None, :]
-    cos, sin = jnp.cos(angles), jnp.sin(angles)
-    return jnp.concatenate([cos, cos], axis=1), jnp.concatenate([-sin, sin], axis=1)
+    sin = jnp.sin(angles)
+    return jnp.cos(angles), jnp.where(lane[None, :] < HEAD // 2, -sin, sin)
 
 
 def local_positions(cp_rank, n_cp, half_len):
@@ -48,6 +50,7 @@
     n_stream = BQ // STREAM
     n_out = y_scr.shape[1] // OUT_COLS
     depth = n_cp * HEAD
+    row_parts = [slice(r, r + half_len) for r in range(0, n_loc, half_len)]
 
     barrier = pltpu.get_barrier_semaphore()
     for other in range(n_cp):
@@ -125,12 +128,13 @@
             par = lax.rem(step, 2)
             for t in range(3):
                 w_copy(g, step, t).wait()
-                prod = jnp.dot(x_scr[...], w_scr[t], preferred_element_type=jnp.float32)
-                for i in range(2):
-                    head = prod[:, i * HEAD:(i + 1) * HEAD]
-                    if t < 2:
-                        head = head * cos_ref[...] + pltpu.roll(head, HEAD // 2, 1) * sin_ref[...]
-                    h_scr[par, i, t] = head.astype(jnp.bfloat16)
+                for rows in row_parts:
+                    prod = jnp.dot(x_scr[rows, :], w_scr[t], preferred_element_type=jnp.float32)
+                    for i in range(2):
+                        head = prod[:, i * HEAD:(i + 1) * HEAD]
+                        if t < 2:
+                            head = head * cos_ref[rows, :] + pltpu.roll(head, HEAD // 2, 1) * sin_ref[rows, :]
+                        h_scr[par, i, t, rows] = head.astype(jnp.bfloat16)
                 later = g * n_chip + step + 1
 
                 @pl.when(later < n_chunk * n_chip)
@@ -156,14 +160,13 @@
 
     def o_send(g, piece):
         dest, half = home(piece)
-        par = lax.rem(g, 2)
         return pltpu.make_async_remote_copy(
-            src_ref=o_scr.at[par, rows_of(piece)], dst_ref=ogot_hbm.at[g, me, pl.ds(half * half_len, half_len)],
-            send_sem=osend_sem.at[par, piece], recv_sem=orecv_sem.at[g, me, half], device_id={'cp': dest}, device_id_type=MESH)
+            src_ref=o_scr.at[g, rows_of(piece)], dst_ref=ogot_hbm.at[g, me, pl.ds(half * half_len, half_len)],
+            send_sem=osend_sem.at[g, piece], recv_sem=orecv_sem.at[g, me, half], device_id={'cp': dest}, device_id_type=MESH)
 
     def o_keep(g, piece):
         dest, half = home(piece)
-        return pltpu.make_async_copy(o_scr.at[lax.rem(g, 2), rows_of(piece)], ogot_hbm.at[g, dest, pl.ds(half * half_len, half_len)], oself_sem.at[half])
+        return pltpu.make_async_copy(o_scr.at[g, rows_of(piece)], ogot_hbm.at[g, dest, pl.ds(half * half_len, half_len)], oself_sem.at[half])
 
     def o_recv(g, src, half):
         return pltpu.make_async_remote_copy(
@@ -215,9 +218,6 @@
         return None if off >= BK - 1 else off
 
     def attend(g):
-        @pl.when(g >= 2)
-        def _():
-            o_sent(g - 2)
         for src in range(n_cp):
             @pl.when(me != src)
             def _():
@@ -225,7 +225,6 @@
         for piece in range(n_pieces):
             for copy in load(g, piece):
                 copy.start()
-        par = lax.rem(g, 2)
 
         @pl.loop(0, seq // BQ)
         def _(qi):
@@ -267,7 +266,7 @@
             for u in range(n_stream):
                 cols = slice(u * STREAM, (u + 1) * STREAM)
                 out = acc_scr[:, cols] / ml_scr[1:2, cols]
-                o_scr[par, pl.ds(q_base + u * STREAM, STREAM), :] = out.T.astype(jnp.bfloat16)
+                o_scr[g, pl.ds(q_base + u * STREAM, STREAM), :] = out.T.astype(jnp.bfloat16)
             for i in range(seq // BQ):
                 @pl.when(qi == i)
                 def _():
@@ -310,7 +309,8 @@
             slot = lax.rem(nb, 2)
             cols = pl.ds(pl.multiple_of(nb * OUT_COLS, OUT_COLS), OUT_COLS)
             wo_copy(g, nb, slot).wait()
-            y_scr[:, cols] += jnp.dot(oc_scr[...], wo_scr[slot], preferred_element_type=jnp.float32)
+            for rows in row_parts:
+                y_scr[rows, cols] += jnp.dot(oc_scr[rows, :], wo_scr[slot], preferred_element_type=jnp.float32)
 
             @pl.when(nb + 2 < n_out)
             def _():
@@ -324,27 +324,16 @@
                 ys_scr[slot] = y_scr[:, cols].astype(jnp.bfloat16)
                 y_copy(nb, slot).start()
 
-    @pl.loop(0, n_chunk + 4)
-    def _(i):
-        @pl.when(i < n_chunk)
-        def _():
-            project(i)
-
-        @pl.when(jnp.logical_and(i >= 2, i < n_chunk + 2))
-        def _():
-            attend(i - 2)
-
-        @pl.when(i >= 4)
-        def _():
-            combine(i - 4)
+    pl.loop(0, n_chunk)(project)
+    pl.loop(0, n_chunk)(attend)
+    pl.loop(0, n_chunk)(combine)
 
     for nb in range(n_out - 2, n_out):
         y_copy(nb, nb % 2).wait()
-    for g in range(max(n_chunk - 2, 0), n_chunk):
-        o_sent(g)
 
     @pl.loop(0, n_chunk)
     def _(g):
+        o_sent(g)
         for dest in range(n_cp):
             @pl.when(me != dest)
             def _():
@@ -373,16 +362,32 @@
                    pieces, pieces, shape((n_chunk, n_cp, n_loc, HEAD), bf16)],
         scratch_shapes=[
             pltpu.VMEM((n_loc, d_model), bf16), pltpu.VMEM((3, d_model, LANES), bf16), pltpu.VMEM((2, 2, 3, n_loc, HEAD), bf16),
-            rows, rows, rows, pltpu.VMEM((HEAD, seq), bf16), pltpu.VMEM((2, seq, HEAD), bf16), pltpu.VMEM((HEAD, BQ), f32),
+            rows, rows, rows, pltpu.VMEM((HEAD, seq), bf16), pltpu.VMEM((n_chunk, seq, HEAD), bf16), pltpu.VMEM((HEAD, BQ), f32),
             stats, stats, score, score,
             pltpu.VMEM((n_loc, n_cp * HEAD), bf16), pltpu.VMEM((2, n_cp * HEAD, OUT_COLS), bf16), pltpu.VMEM((n_loc, w_o.shape[1]), f32),
             pltpu.VMEM((2, n_loc, OUT_COLS), bf16),
             dma, dma((3,)), dma((2, 2, 3)), dma((n_chunk, n_cp)), dma((n_chunk, n_cp)), dma((2 * n_cp, 3)), dma((2,)),
-            dma((2, 2 * n_cp)), dma((n_chunk, n_cp, 2)), dma((n_cp,)), dma((2,)), dma((2,))],
-        compiler_params=pltpu.CompilerParams(collective_id=0, has_side_effects=True, vmem_limit_bytes=62 << 20),
+            dma((n_chunk, 2 * n_cp)), dma((n_chunk, n_cp, 2)), dma((n_cp,)), dma((2,)), dma((2,))],
+        compiler_params=pltpu.CompilerParams(collective_id=0, has_side_effects=True, vmem_limit_bytes=67043328),
         name="layer",
     )(x_loc, w_q, w_k, w_v, w_o, cos, sin)
     return y, k_plain, v_plain
+
+
+def split_heads_kernel(k_ref, v_ref, k_out, v_out):
+    k_out[...] = k_ref[...].reshape(k_out.shape)
+    v_out[...] = v_ref[...].reshape(v_out.shape)
+
+
+def split_heads(k_plain, v_plain):
+    n_loc, width = k_plain.shape
+    flat = pl.BlockSpec((COPY_ROWS, width), lambda i: (i, 0))
+    split = pl.BlockSpec((COPY_ROWS, width // HEAD, HEAD), lambda i: (i, 0, 0))
+    out = jax.ShapeDtypeStruct((n_loc, width // HEAD, HEAD), k_plain.dtype)
+    return pl.pallas_call(
+        split_heads_kernel, grid=(n_loc // COPY_ROWS,), in_specs=[flat, flat], out_specs=[split, split], out_shape=[out, out],
+        compiler_params=pltpu.CompilerParams(vmem_limit_bytes=40 << 20), name="split_heads",
+    )(k_plain, v_plain)
 
 
 def solution(mesh):
@@ -392,7 +397,7 @@
         n_loc = x_loc.shape[0]
         cos, sin = rope_tables(local_positions(lax.axis_index('cp'), n_cp, n_loc // 2))
         y_loc, k_plain, v_plain = layer(x_loc, w_q, w_k, w_v, w_o, cos, sin, n_cp)
-        return y_loc, k_plain.reshape(n_loc, -1, HEAD), v_plain.reshape(n_loc, -1, HEAD)
+        return y_loc, *split_heads(k_plain, v_plain)
 
     row_spec = P(('dp', 'cp'), None)
     kv_spec = P(('dp', 'cp'), None, None)

time: 462 us -> 403 us (0.87)
  Pallas kernels: 436 us -> 393 us
  local copies, waits for them, and re-layouts: 21.1 us -> 6.45 us
    pallas_call x1, Pallas kernels: 436 us -> 381 us  [layer(): pl.pallas_call(functools.partial(layer_kernel, n_cp, n_chunk), in_specs=[...]
    unnamed x7 -> x5, local copies, waits for them, and re-layouts: 21.1 us -> 6.45 us
    pallas_call x0 -> x1, Pallas kernels: none -> 11.5 us  [split_heads(): pl.pallas_call(split_heads_kernel, grid=(n_loc // COPY_ROWS,), in_specs=[...]
where the time goes in v2:
time: 403 us; the launch traced here: 402 us
  Pallas kernels  393 us (98%)
  local copies, waits for them, and re-layouts  6.45 us (2%)
    pallas_call x1, Pallas kernels, layer(): pl.pallas_call(functools.partial(layer_kernel, n_cp, n_chunk), in_specs=[...  381 us
    pallas_call x1, Pallas kernels, split_heads(): pl.pallas_call(split_heads_kernel, grid=(n_loc // COPY_ROWS,), in_specs=[...  11.5 us

profile of v2, /device:TPU:112, one launch (start us, length us, event | category | flops | bytes accessed | tf_op | source)
XLA Modules:
  0.0 402.4 jit_solution(13494351835943783510)
XLA Ops:
  0.7 2.5 negate_select_fusion
  3.2 381.2 %layer.1 = (bf16[768,5120]{1,0:T(8,128)(2,1)}, bf16[768,5120]{1,0:T(8,128)(2,1)}, bf16[768,5120]{1,0:T(8,128)(2,1)}, bf16[5,8,3,768,128]{4,3,2,1,0:T(8,128)(2,1)...) custom-call(bf16[768,5120]{1,0:T(8,128)(2,1)} %x_hbm.1, bf16[5120,5120]{1,0:T(8,128)(2,1)} %wq_hbm.1, ...), custom_call_target="tpu_custom_call" | custom-call | tf_op jit(solution)/shard_map/layer/pallas_call | solution.py:357
  384.4 0.0 copy-start
  384.4 3.2 copy-done
  387.6 0.0 copy-start.1
  387.6 11.5 %split_heads.1 = (bf16[768,40,128]{2,1,0:T(8,128)(2,1)}, bf16[768,40,128]{2,1,0:T(8,128)(2,1)}) custom-call(bf16[768,5120]{1,0:T(8,128)(2,1)S(1)} %copy-done, bf16[768,5120]{1,0:T(8,128)(2,1)} %get-tuple-element.10.v_ref), custom_call_target="tpu_custom_call" | custom-call | tf_op jit(solution)/shard_map/split_heads/pallas_call | solution.py:387
  399.2 0.0 copy-done.1
  399.2 3.2 copy.9
  (4 shorter events, 0.0 us)
Async XLA Ops:
  384.4 3.2 copy-start
  387.6 11.6 %copy-start.1 = (bf16[768,5120]{1,0:T(8,128)(2,1)S(1)}, bf16[768,5120]{1,0:T(8,128)(2,1)}, u32[]{:S(2)}) copy-start(bf16[768,5120]{1,0:T(8,128)(2,1)} %get-tuple-element.20) | copy-start | bytes 23592964
